TPU v7x, 32 devices: a whole 2x2x4 slice. The times are simulated.
32 devices in a mesh: row: 2 (over x), col: 16 (over z, y, core).
Axes of the slice: x: 2, y: 2, z: 4, core: 2. Of those that a mesh axis runs over, the one named last changes fastest.
Arguments:
- ld_matrix: bfloat16 [32768, 32768], P('row', 'col'), may hold values from -0.23925781 to 0.23925781
- factor: float32 [32768, 256], P(('row', 'col')), may hold values from -0.24 to 0.24
- diag_values: bfloat16 [32768], P('col'), may hold values from 0.5 to 4
Outputs:
- factor_grad: float32 [32768, 256], P(('row', 'col'))
All inputs are finite; a program needn't handle non-finite values.
Results may differ from a plain program's by a relative error of at most 0.003.
Values may be sent and summed in bfloat16 or wider, within the bound.
A program may use at most 128 MiB of HBM per device.

v0:
```python
import functools

import jax
import jax.numpy as jnp
from jax import lax
from jax.experimental import pallas as pl
from jax.experimental.pallas import tpu as pltpu
from jax.sharding import PartitionSpec as P

MESH = pl.DeviceIdType.MESH
F32, BF16 = jnp.float32, jnp.bfloat16
TILES = 3


def other(index, stride):
    return index + stride * (1 - 2 * (index // stride % 2))


def kernel(
    n_row, n_col, ld_ref, fac_ref, diag_ref, out_ref,
    tile, panel, keep, s1, r1, s2, r2, s3, r3, gsum, grecv,
    tile_sem, self_sem, p_send, p_recv,
    s1_send, s1_recv, s2_send, s2_recv, s3_send, s3_recv, g_send, g_recv,
):
    r, c = lax.axis_index("row"), lax.axis_index("col")
    own = fac_ref.shape[0]
    n_hi = n_col // 4
    steps = 2 * n_hi
    chunk = min(256, own)
    b0, b1, hi = c % 2, c // 2 % 2, c // 4

    def remote(src, dst, send, recv, row, col):
        return pltpu.make_async_remote_copy(
            src_ref=src, dst_ref=dst, send_sem=send, recv_sem=recv,
            device_id=(row, col), device_id_type=MESH,
        )

    def shard_of(u):
        t, side = u // 2, u % 2
        h = (hi + 1 + t) % n_hi
        mid = (b1 + 1 + t // n_hi) % 2
        return 4 * h + 2 * mid + (b0 + 1 + side) % 2

    def fetch(u):
        rows = pl.ds(pl.multiple_of(shard_of(u) * own, own), own)
        return pltpu.make_async_copy(ld_ref.at[rows], tile.at[u % TILES], tile_sem.at[u % TILES])

    for u in range(TILES - 1):
        fetch(jnp.int32(u)).start()

    mine = r * n_col + c
    to_col, to_slot = mine // n_row, mine % n_row

    def panel_at(j):
        return panel.at[pl.ds(pl.multiple_of(j * own, own), own)]

    def to_row(k):
        return remote(
            fac_ref, panel_at(to_slot), p_send.at[k], p_recv.at[to_slot], (r + k) % n_row, to_col
        )

    local_copy = pltpu.make_async_copy(fac_ref, panel_at(to_slot), self_sem)
    home = to_col == c

    @pl.when(home)
    def _():
        local_copy.start()

    @pl.when(jnp.logical_not(home))
    def _():
        to_row(0).start()

    for k in range(1, n_row):
        to_row(k).start()

    for j in range(n_row):
        @pl.when(n_row * c + j != mine)
        def _():
            remote(fac_ref, panel_at(j), p_send.at[0], p_recv.at[j], r, c).wait_recv()

        @pl.when(n_row * c + j == mine)
        def _():
            local_copy.wait()

    gsum[0] = lax.dot_general(
        panel[...], panel[...], (((0,), (0,)), ((), ())), preferred_element_type=F32
    )
    strides = [1] + [2 ** b for b in range(2, n_col.bit_length() - 1)] + [2]

    def gram_copy(e):
        return remote(
            gsum.at[e], grecv.at[e], g_send.at[e], g_recv.at[e], r, other(c, strides[e])
        )

    def first(t):
        return remote(s1.at[t], r1.at[t], s1_send.at[t], s1_recv.at[t], r, other(c, 1))

    def second(t):
        return remote(s2.at[t], r2.at[t], s2_send.at[t], s2_recv.at[t], r, other(c, 2))

    def third(k):
        return remote(
            s3.at[k], r3.at[k], s3_send.at[k], s3_recv.at[k], r, (hi + 1 + k) % n_hi * 4 + c % 4
        )

    def compute(u, store):
        @pl.when(u + TILES - 1 < 2 * steps)
        def _():
            fetch(u + TILES - 1).start()

        fetch(u).wait()
        j = r * n_col + shard_of(u) - n_row * c
        inside = jnp.where((j >= 0) & (j < n_row), 1.0, 0.0).astype(F32)
        base = jnp.clip(j, 0, n_row - 1) * own

        @pl.loop(0, own // chunk)
        def _(m):
            rows = pl.ds(pl.multiple_of(m * chunk, chunk), chunk)
            diag_rows = pl.ds(pl.multiple_of(base + m * chunk, chunk), chunk)
            acc = jnp.dot(tile[u % TILES, rows, :], panel[...], preferred_element_type=F32)
            acc -= inside * diag_ref[diag_rows, :] * panel[diag_rows, :].astype(F32)
            store(rows, acc)

    def pass_on(t):
        first(t).wait_recv()
        s2[t] = (keep[t] + r1[t].astype(F32)).astype(BF16)
        second(t).start()

    @pl.loop(0, steps)
    def _(t):
        def to_partner(rows, acc):
            s1[t, rows, :] = acc.astype(BF16)

        def to_keep(rows, acc):
            keep[t, rows, :] = acc

        compute(2 * t, to_partner)
        first(t).start()
        compute(2 * t + 1, to_keep)

        @pl.when((t >= 1) & (t <= n_hi))
        def _():
            pass_on(t - 1)

        for e in range(len(strides)):
            @pl.when(t == e)
            def _():
                if e > 0:
                    gram_copy(e - 1).wait_recv()
                    gsum[e] = gsum[e - 1] + grecv[e - 1]
                gram_copy(e).start()

    @pl.loop(0, n_hi - 1)
    def _(k):
        first(n_hi + k).wait_recv()
        second(k).wait_recv()
        s3[k] = (keep[n_hi + k] + r1[n_hi + k].astype(F32) + r2[k].astype(F32)).astype(BF16)
        third(k).start()

    last = len(strides) - 1
    gram_copy(last).wait_recv()
    gram = gsum[last] + grecv[last]
    gram_hi = gram.astype(BF16)
    gram_lo = (gram - gram_hi.astype(F32)).astype(BF16)
    first(steps - 1).wait_recv()
    second(n_hi - 1).wait_recv()

    @pl.loop(0, own // chunk)
    def _(m):
        rows = pl.ds(pl.multiple_of(m * chunk, chunk), chunk)
        fac = fac_ref[rows, :]
        model = jnp.dot(fac, gram_hi, preferred_element_type=F32)
        model += jnp.dot(fac, gram_lo, preferred_element_type=F32)
        model -= keep[steps - 1, rows, :] + r1[steps - 1, rows, :].astype(F32)
        out_ref[rows, :] = model - r2[n_hi - 1, rows, :].astype(F32)

    @pl.loop(0, n_hi - 1)
    def _(k):
        third(k).wait_recv()
        out_ref[...] -= r3[k].astype(F32)

    out_ref[...] = 4.0 * out_ref[...]

    @pl.when(jnp.logical_not(home))
    def _():
        to_row(0).wait_send()

    for k in range(1, n_row):
        to_row(k).wait_send()
    for e in range(len(strides)):
        gram_copy(e).wait_send()

    @pl.loop(0, steps)
    def _(t):
        first(t).wait_send()

    @pl.loop(0, n_hi)
    def _(t):
        second(t).wait_send()

    @pl.loop(0, n_hi - 1)
    def _(k):
        third(k).wait_send()


def local(ld_matrix, factor, diag_values):
    n_row, n_col = lax.axis_size("row"), lax.axis_size("col")
    own, rank = factor.shape
    width = ld_matrix.shape[1]
    n_hi = n_col // 4
    steps = 2 * n_hi
    bits = n_col.bit_length() - 1
    dma = lambda *shape: pltpu.SemaphoreType.DMA(shape)
    shards = lambda n: pltpu.VMEM((n, own, rank), BF16)
    vmem = pl.BlockSpec(memory_space=pltpu.VMEM)
    return pl.pallas_call(
        functools.partial(kernel, n_row, n_col),
        out_shape=jax.ShapeDtypeStruct((own, rank), F32),
        in_specs=[pl.BlockSpec(memory_space=pl.ANY), vmem, vmem],
        out_specs=vmem,
        scratch_shapes=[
            pltpu.VMEM((TILES, own, width), BF16),
            pltpu.VMEM((width, rank), BF16),
            pltpu.VMEM((steps, own, rank), F32),
            shards(steps), shards(steps), shards(n_hi), shards(n_hi),
            shards(n_hi - 1), shards(n_hi - 1),
            pltpu.VMEM((bits, rank, rank), F32),
            pltpu.VMEM((bits, rank, rank), F32),
            dma(TILES), pltpu.SemaphoreType.DMA, dma(n_row), dma(n_row),
            dma(steps), dma(steps), dma(n_hi), dma(n_hi),
            dma(n_hi - 1), dma(n_hi - 1), dma(bits), dma(bits),
        ],
        compiler_params=pltpu.CompilerParams(
            has_side_effects=True, vmem_limit_bytes=60 * 2**20
        ),
    )(ld_matrix, factor.astype(BF16), diag_values.astype(F32)[:, None])


def solution(mesh):
    in_specs = (P("row", "col"), P(("row", "col"), None), P("col"))
    out_specs = P(("row", "col"), None)
    return jax.shard_map(local, mesh=mesh, in_specs=in_specs, out_specs=out_specs, check_vma=False)
```

profile of v0, /device:TPU:29, one launch (start us, length us, event | category | flops | bytes accessed | tf_op | source)
XLA Modules:
  0.0 149.0 jit_solution(1916484579154373417)
XLA Ops:
  0.0 0.7 broadcast_in_dim.7
  0.7 2.1 %convert_element_type.4.fac_ref = bf16[1024,256]{1,0:T(8,128)(2,1)} convert(f32[1024,256]{1,0:T(8,128)} %param.4) | non-fusion elementwise | flops 262144 | bytes 1572864 | tf_op jit(solution)/shard_map/convert_element_type | solution.py:236
  2.8 1.3 copy.4.diag_ref
  4.1 142.6 %shard_map.37 = f32[1024,256]{1,0:T(8,128)} custom-call(bf16[16384,2048]{1,0:T(8,128)(2,1)} %ld_ref.1, bf16[1024,256]{1,0:T(8,128)(2,1)} %convert_element_type.4.fac_ref, f32[2048,1]{1,0:T(8,128)} %copy.4.diag_ref), custom_call_target="tpu_custom_call" | custom-call | tf_op jit(solution)/shard_map/pallas_call | solution.py:216
  146.8 2.3 %copy.6 = f32[1024,256]{1,0:T(8,128)} copy(f32[1024,256]{1,0:T(8,128)} %shard_map.37) | data formatting | bytes 2097152
where the time goes:
time: 149 us
  Pallas kernels  143 us (96%)
  local copies, waits for them, and re-layouts  3.61 us (2%)
  other arithmetic  2.78 us (2%)
    pallas_call x1, Pallas kernels, local(): pl.pallas_call(functools.partial(kernel, n_row, n_col), out_shape=jax.Sha...  143 us

commit v1 on v0

v1 whole, which is shorter than its diff:
```python
import functools

import jax
import jax.numpy as jnp
from jax import lax
from jax.experimental import pallas as pl
from jax.experimental.pallas import tpu as pltpu
from jax.sharding import PartitionSpec as P

MESH = pl.DeviceIdType.MESH
F32, BF16 = jnp.float32, jnp.bfloat16
CHUNK = 256
LAG = 3
PIECES = 2
LANES = 128


def rows_at(start, count):
    return pl.ds(pl.multiple_of(start, count), count)


def flip(index, stride):
    return index + stride * (1 - 2 * (index // stride % 2))


def kernel(
    n_row, n_col, tiles, ld_ref, f32_ref, diag_ref, out_ref,
    tile, fac, panel, stage, keep, s1, r1, s2, r2, s3, r3, gsum, grecv, gfull,
    tile_sem, a_send, b_send, b_recv, c_send, line_recv, x_send, x_recv,
    s1_send, s1_recv, s2_send, s2_recv, s3_send, s3_recv, g_send, g_recv,
):
    r, c = lax.axis_index("row"), lax.axis_index("col")
    own, rank = fac.shape
    n_hi = n_col // 4
    chunk = s2.shape[1]
    nm = own // chunk
    steps = n_hi * nm
    far = (n_hi - 1) * nm
    core, mid, hi = c % 2, c // 2 % 2, c // 4
    half = rank // 2

    def remote(src, dst, send, recv, row, col):
        return pltpu.make_async_remote_copy(
            src_ref=src, dst_ref=dst, send_sem=send, recv_sem=recv,
            device_id=(row, col), device_id_type=MESH,
        )

    mirrored = hi >= n_hi // 2
    near = jnp.where(mirrored, n_hi - 1 - hi, hi)

    def target(t):
        ahead = n_hi - 1 - t
        behind = t - (n_hi - 1 - near)
        other = jnp.where(t < n_hi - 1 - near, ahead, behind)
        tgt = jnp.where(t == n_hi - 1, near, other)
        return jnp.where(mirrored, n_hi - 1 - tgt, tgt)

    def shard_of(v):
        t, side, which = v // 4 // nm, v // 2 % 2, v % 2
        return 4 * target(t) + 2 * ((mid + 1 + side) % 2) + (core + 1 + which) % 2

    def fetch(v):
        start = shard_of(v) * own + v // 4 % nm * chunk
        return pltpu.make_async_copy(
            ld_ref.at[rows_at(start, chunk)], tile.at[v % tiles], tile_sem.at[v % tiles]
        )

    @pl.loop(0, tiles)
    def _(v):
        fetch(v).start()

    fac[...] = f32_ref[...].astype(BF16)
    mine = r * n_col + c

    def panel_rows(slot, start, count):
        return panel.at[rows_at(slot * own + start, count)]

    if n_row == 2:
        part = own // 2 // PIECES
        x_col = c

        def b_copy(p):
            return remote(
                fac.at[pl.ds(own // 2 + p * part, part)], stage.at[p],
                b_send.at[p], b_recv.at[p], 1 - r, x_col,
            )

        slot = mine % n_row
        a_col = mine // n_row
        c_col = ((1 - r) * n_col + c) // n_row
        c_slot = ((1 - r) * n_col + c) % n_row

        def a_copy(p):
            return remote(
                fac.at[pl.ds(p * part, part)], panel_rows(slot, p * part, part),
                a_send.at[p], line_recv.at[slot, p], r, a_col,
            )

        def c_copy(p):
            return remote(
                stage.at[p], panel_rows(c_slot, own // 2 + p * part, part),
                c_send.at[p], line_recv.at[c_slot, p], r, c_col,
            )

        source_row = n_row * c // n_col
        line_half = jnp.where(source_row == r, 0, own // 2)

        def line_wait(j, p):
            remote(
                stage.at[0], panel_rows(j, line_half + p * part, part),
                c_send.at[0], line_recv.at[j, p], r, c,
            ).wait_recv()

        def x_copy(j, p):
            piece = panel_rows(j, line_half + p * part, part)
            return remote(piece, piece, x_send.at[j, p], x_recv.at[j, p], 1 - r, c)

        def x_wait(j, p):
            piece = panel_rows(j, own // 2 - line_half + p * part, part)
            remote(piece, piece, x_send.at[j, p], x_recv.at[j, p], 1 - r, c).wait_recv()

        for p in range(PIECES):
            b_copy(p).start()

        @pl.when(a_col != c)
        def _():
            for p in range(PIECES):
                a_copy(p).start()

        @pl.when(a_col == c)
        def _():
            panel_rows(slot, 0, own // 2)[...] = fac[: own // 2, :]
    else:
        to_col, to_slot = mine // n_row, mine % n_row

        def to_row(k):
            return remote(
                fac, panel_rows(to_slot, 0, own), a_send.at[k], x_recv.at[0, to_slot],
                (r + k) % n_row, to_col,
            )

        home = to_col == c

        @pl.when(home)
        def _():
            panel_rows(to_slot, 0, own)[...] = fac[...]

        @pl.when(jnp.logical_not(home))
        def _():
            to_row(0).start()

        for k in range(1, n_row):
            to_row(k).start()

    gram = lax.dot_general(
        fac[...], fac[...], (((0,), (0,)), ((), ())), preferred_element_type=F32
    )
    gfull[...] = gram
    col_strides = [2 ** b for b in range(1, n_col.bit_length() - 1)]
    row_strides = [2 ** b for b in range(n_row.bit_length() - 1)]
    links = [("col", s) for s in col_strides] + [("row", s) for s in row_strides]
    n_ex = len(links) + 2

    def gram_half(which):
        return gfull.at[rows_at(which * half, half)]

    def gram_copy(e):
        if e == 0:
            src, row, col = gram_half(1 - core), r, flip(c, 1)
        elif e == n_ex - 1:
            src, row, col = gsum.at[e - 1], r, flip(c, 1)
        else:
            axis, stride = links[e - 1]
            src = gsum.at[e - 1]
            row = flip(r, stride) if axis == "row" else r
            col = flip(c, stride) if axis == "col" else c
        return remote(src, grecv.at[e], g_send.at[e], g_recv.at[e], row, col)

    def gram_step(e):
        gram_copy(e - 1).wait_recv()
        before = gram_half(core)[...] if e == 1 else gsum[e - 2]
        gsum[e - 1] = before + grecv[e - 1]
        gram_copy(e).start()

    gram_copy(0).start()

    if n_row == 2:
        for p in range(PIECES):
            b_copy(p).wait_recv()

            @pl.when(c_col != c)
            def _():
                c_copy(p).start()

            @pl.when(c_col == c)
            def _():
                panel_rows(c_slot, own // 2 + p * part, part)[...] = stage[p]

        gram_step(1)
        for p in range(PIECES):
            for j in range(n_row):
                @pl.when((n_row * c + j) % n_col != c)
                def _():
                    line_wait(j, p)

                x_copy(j, p).start()
        for p in range(PIECES):
            for j in range(n_row):
                x_wait(j, p)
    else:
        gram_step(1)
        for j in range(n_row):
            @pl.when(n_row * c + j != mine)
            def _():
                remote(
                    fac, panel_rows(j, 0, own), a_send.at[0], x_recv.at[0, j], r, c
                ).wait_recv()

    def first(u):
        return remote(s1.at[u], r1.at[u], s1_send.at[u], s1_recv.at[u], r, flip(c, 1))

    def second(i):
        return remote(s2.at[i], r2.at[i], s2_send.at[i], s2_recv.at[i], r, flip(c, 2))

    def third(j, way, tgt, m):
        col = jnp.where(way == 0, c + 4, c - 4)
        return remote(
            s3.at[j], r3.at[way, tgt, m], s3_send.at[j], s3_recv.at[way, tgt, m], r, col
        )

    def compute(v):
        fetch(v).wait()
        acc = jnp.dot(tile[v % tiles], panel[...], preferred_element_type=F32)

        @pl.when(v + tiles < 4 * steps)
        def _():
            fetch(v + tiles).start()

        return acc

    def diagonal(v, ref):
        j = r * n_col + shard_of(v) - n_row * c

        @pl.when((j >= 0) & (j < n_row))
        def _():
            base = j * own + v // 4 % nm * chunk
            line = lax.broadcasted_iota(jnp.int32, (LANES, LANES), 0)
            lane = lax.broadcasted_iota(jnp.int32, (LANES, LANES), 1)
            for q in range(chunk // LANES):
                at = rows_at(base + q * LANES, LANES)
                values = jnp.broadcast_to(diag_ref[:, at].astype(F32), (LANES, LANES))
                square = jnp.where(line == lane, values, 0.0).astype(BF16)
                ref[pl.ds(q * LANES, LANES), :] -= jnp.dot(
                    square, panel[at, :], preferred_element_type=F32
                )

    def to_next(j):
        t, m = j // nm, j % nm
        tgt = target(t)
        way = jnp.where(tgt > hi, 0, 1)
        inner = jnp.where(way == 0, hi, n_hi - 1 - hi) > 0
        first(2 * j + 1).wait_recv()
        second(j).wait_recv()
        acc = keep[2 * j + 1] + r1[2 * j + 1].astype(F32) + r2[j].astype(F32)

        @pl.when(inner)
        def _():
            third(j, way, tgt, m).wait_recv()
            s3[j] = (acc + r3[way, tgt, m].astype(F32)).astype(BF16)

        @pl.when(jnp.logical_not(inner))
        def _():
            s3[j] = acc.astype(BF16)

        third(j, way, tgt, m).start()

    @pl.loop(0, steps)
    def _(i):
        for side in range(2):
            u = 2 * i + side
            scratch = keep.at[2 * steps]
            scratch[...] = compute(2 * u)
            diagonal(2 * u, scratch)
            s1[u] = scratch[...].astype(BF16)
            first(u).start()
            keep[u] = compute(2 * u + 1)
            diagonal(2 * u + 1, keep.at[u])
        first(2 * i).wait_recv()
        s2[i] = (keep[2 * i] + r1[2 * i].astype(F32)).astype(BF16)
        second(i).start()

        @pl.when((i >= LAG) & (i - LAG < far))
        def _():
            to_next(i - LAG)

        for e in range(2, n_ex):
            if e - 1 < steps:
                @pl.when(i == e - 1)
                def _():
                    gram_step(e)

    for e in range(max(2, steps + 1), n_ex):
        gram_step(e)

    if steps - LAG < far:
        @pl.loop(max(steps - LAG, 0), far)
        def _(j):
            to_next(j)

    gram_copy(n_ex - 1).wait_recv()
    gram_copy(0).wait_send()
    gram_half(core)[...] = gsum[n_ex - 2]
    gram_half(1 - core)[...] = grecv[n_ex - 1]
    total = gfull[...]
    total_hi = total.astype(BF16)
    total_lo = (total - total_hi.astype(F32)).astype(BF16)

    @pl.loop(0, nm)
    def _(m):
        rows = rows_at(m * chunk, chunk)
        model = jnp.dot(fac[rows, :], total_hi, preferred_element_type=F32)
        model += jnp.dot(fac[rows, :], total_lo, preferred_element_type=F32)
        out_ref[rows, :] = model

    @pl.loop(0, nm)
    def _(m):
        j = far + m
        rows = rows_at(m * chunk, chunk)
        first(2 * j + 1).wait_recv()
        out_ref[rows, :] -= keep[2 * j + 1] + r1[2 * j + 1].astype(F32)

        @pl.when(hi > 0)
        def _():
            third(0, 0, hi, m).wait_recv()
            out_ref[rows, :] -= r3[0, hi, m].astype(F32)

        @pl.when(hi < n_hi - 1)
        def _():
            third(0, 1, hi, m).wait_recv()
            out_ref[rows, :] -= r3[1, hi, m].astype(F32)

        second(j).wait_recv()
        out_ref[rows, :] = 4.0 * (out_ref[rows, :] - r2[j].astype(F32))

    if n_row == 2:
        for p in range(PIECES):
            b_copy(p).wait_send()

            @pl.when(a_col != c)
            def _():
                a_copy(p).wait_send()

            @pl.when(c_col != c)
            def _():
                c_copy(p).wait_send()

            for j in range(n_row):
                x_copy(j, p).wait_send()
    else:
        @pl.when(jnp.logical_not(home))
        def _():
            to_row(0).wait_send()

        for k in range(1, n_row):
            to_row(k).wait_send()
    for e in range(1, n_ex):
        gram_copy(e).wait_send()

    @pl.loop(0, steps)
    def _(i):
        first(2 * i).wait_send()
        first(2 * i + 1).wait_send()
        second(i).wait_send()

    @pl.loop(0, far)
    def _(j):
        tgt = target(j // nm)
        third(j, jnp.where(tgt > hi, 0, 1), tgt, j % nm).wait_send()


def local(ld_matrix, factor, diag_values):
    n_row, n_col = lax.axis_size("row"), lax.axis_size("col")
    own, rank = factor.shape
    width = ld_matrix.shape[1]
    n_hi = n_col // 4
    chunk = min(CHUNK, own)
    nm = own // chunk
    steps = n_hi * nm
    far = (n_hi - 1) * nm
    tiles = min(22, 4 * steps)
    n_ex = n_col.bit_length() - 2 + n_row.bit_length() - 1 + 2
    dma = lambda *shape: pltpu.SemaphoreType.DMA(shape)
    sums = lambda *n: pltpu.VMEM((*n, chunk, rank), BF16)
    gram = pltpu.VMEM((n_ex, rank // 2, rank), F32)
    vmem = pl.BlockSpec(memory_space=pltpu.VMEM)
    pieces = max(PIECES, n_row)
    return pl.pallas_call(
        functools.partial(kernel, n_row, n_col, tiles),
        out_shape=jax.ShapeDtypeStruct((own, rank), F32),
        in_specs=[pl.BlockSpec(memory_space=pl.ANY), vmem, vmem],
        out_specs=vmem,
        scratch_shapes=[
            pltpu.VMEM((tiles, chunk, width), BF16),
            pltpu.VMEM((own, rank), BF16),
            pltpu.VMEM((width, rank), BF16),
            pltpu.VMEM((PIECES, own // 2 // PIECES, rank), BF16),
            pltpu.VMEM((2 * steps + 1, chunk, rank), F32),
            sums(2 * steps), sums(2 * steps), sums(steps), sums(steps),
            sums(far), sums(2, n_hi, nm),
            gram, gram, pltpu.VMEM((rank, rank), F32),
            dma(tiles), dma(pieces), dma(PIECES), dma(PIECES), dma(PIECES),
            dma(n_row, PIECES), dma(n_row, pieces), dma(n_row, pieces),
            dma(2 * steps), dma(2 * steps), dma(steps), dma(steps),
            dma(far), dma(2, n_hi, nm), dma(n_ex), dma(n_ex),
        ],
        compiler_params=pltpu.CompilerParams(
            has_side_effects=True, vmem_limit_bytes=62 * 2**20
        ),
    )(ld_matrix, factor, diag_values[None, :])


def solution(mesh):
    in_specs = (P("row", "col"), P(("row", "col"), None), P("col"))
    out_specs = P(("row", "col"), None)
    return jax.shard_map(local, mesh=mesh, in_specs=in_specs, out_specs=out_specs, check_vma=False)
```

time: 149 us -> 99.8 us (0.67)
  the two profiles are of different devices: /device:TPU:29 before, /device:TPU:0 now
where the time goes in v1:
time: 99.8 us; the launch traced here: 98.8 us
  Pallas kernels  95.2 us (95%)
  local copies, waits for them, and re-layouts  3.55 us (4%)
    pallas_call x1, Pallas kernels, local(): pl.pallas_call(functools.partial(kernel, n_row, n_col, tiles), out_shape=...  95.2 us
    unnamed x1, local copies, waits for them, and re-layouts  2.26 us

profile of v1, /device:TPU:0, one launch (start us, length us, event | category | flops | bytes accessed | tf_op | source)
XLA Modules:
  0.0 98.8 jit_solution(10977527656264079925)
XLA Ops:
  0.0 1.3 %broadcast_in_dim.3.diag_ref = bf16[1,2048]{1,0:T(2,128)(2,1)} reshape(bf16[2048]{0:T(1024)(128)(2,1)} %param.5) | data formatting | bytes 8192 | tf_op jit(solution)/shard_map/broadcast_in_dim | solution.py:419
  1.3 95.2 %shard_map.37 = f32[1024,256]{1,0:T(8,128)} custom-call(bf16[16384,2048]{1,0:T(8,128)(2,1)} %ld_ref.1, f32[1024,256]{1,0:T(8,128)} %f32_ref.1, bf16[1,2048]{1,0:T(2,128)(2,1)} %broadcast_in_dim.3.diag_ref), custom_call_target="tpu_custom_call" | custom-call | tf_op jit(solution)/shard_map/pallas_call | solution.py:397
  96.5 2.3 %copy.5 = f32[1024,256]{1,0:T(8,128)} copy(f32[1024,256]{1,0:T(8,128)} %shard_map.37) | data formatting | bytes 2097152

commit v2 on v1

v2 whole, which is shorter than its diff:
```python
import functools

import jax
import jax.numpy as jnp
from jax import lax
from jax.experimental import pallas as pl
from jax.experimental.pallas import tpu as pltpu
from jax.sharding import PartitionSpec as P

MESH = pl.DeviceIdType.MESH
F32, BF16 = jnp.float32, jnp.bfloat16
CHUNK = 256
LAG = 3
PACE = 3
SLOTS = 6
PARTS = 16
ALONE = 4
LANES = 128


def rows_at(start, count):
    return pl.ds(pl.multiple_of(start, count), count)


def flip(index, stride):
    return index + stride * (1 - 2 * (index // stride % 2))


def kernel(
    n_row, n_col, slots, ld_ref, f32_ref, diag_ref, out_ref,
    tile, wide, fac, diag, panel, stage, acc, keep, result,
    s1, r1, s2, r2, s3, r3, gsum, grecv, gfull,
    tile_sem, in_sem, out_sem, a_send, b_send, b_recv, c_send, line_recv, x_send, x_recv,
    s1_send, s1_recv, s2_send, s2_recv, s3_send, s3_recv, g_send, g_recv,
):
    r, c = lax.axis_index("row"), lax.axis_index("col")
    own, rank = fac.shape
    n_hi = n_col // 4
    chunk = s2.shape[1]
    nm = own // chunk
    steps = n_hi * nm
    far = (n_hi - 1) * nm
    core, mid, hi = c % 2, c // 2 % 2, c // 4
    half = rank // 2
    part = own // PARTS
    mine = r * n_col + c
    col_strides = [2 ** b for b in range(1, n_col.bit_length() - 1)]
    row_strides = [2 ** b for b in range(n_row.bit_length() - 1)]

    def remote(src, dst, send, recv, row, col):
        return pltpu.make_async_remote_copy(
            src_ref=src, dst_ref=dst, send_sem=send, recv_sem=recv,
            device_id=(row, col), device_id_type=MESH,
        )

    a_col, a_slot = mine // n_row, mine % n_row
    twin = (1 - r) * n_col + c
    c_col, c_slot = twin // n_row, twin % n_row

    if n_row == 2:
        barrier = pltpu.get_barrier_semaphore()
        greeted = [(r, flip(c, s)) for s in [1] + col_strides] + [(1 - r, c)]
        greeted += [(r, col) for col in (a_col, c_col, 2 * c % n_col, (2 * c + 1) % n_col)]
        greeted += [(r, jnp.where(hi < n_hi - 1, c + 4, c)), (r, jnp.where(hi > 0, c - 4, c))]
        others = [jnp.where((row != r) | (col != c), 1, 0) for row, col in greeted]
        for (row, col), other in zip(greeted, others):
            @pl.when(other == 1)
            def _():
                pl.semaphore_signal(barrier, inc=1, device_id=(row, col), device_id_type=MESH)

    load = pltpu.make_async_copy(f32_ref, wide, in_sem)
    load.start()

    mirrored = hi >= n_hi // 2
    near = jnp.where(mirrored, n_hi - 1 - hi, hi)

    def target(t):
        ahead = n_hi - 1 - t
        behind = t - (n_hi - 1 - near)
        other = jnp.where(t < n_hi - 1 - near, ahead, behind)
        tgt = jnp.where(t == n_hi - 1, near, other)
        return jnp.where(mirrored, n_hi - 1 - tgt, tgt)

    def shard_of(i, side, which):
        return 4 * target(i // nm) + 2 * ((mid + 1 + side) % 2) + (core + 1 + which) % 2

    def fetch(i, side, which):
        start = shard_of(i, side, which) * own + i % nm * chunk
        return pltpu.make_async_copy(
            ld_ref.at[rows_at(start, chunk)],
            tile.at[i % slots, side, pl.ds(which * chunk, chunk)],
            tile_sem.at[i % slots, side, which],
        )

    @pl.loop(0, slots)
    def _(i):
        for side in range(2):
            for which in range(2):
                fetch(i, side, which).start()

    diag[...] = diag_ref[...].astype(F32)
    load.wait()
    fac[...] = wide[...].astype(BF16)

    links = [("col", 1), ("col", 2), ("row", 1)]
    links += [("col", s) for s in col_strides[1:]] + [("row", s) for s in row_strides[1:]]
    links += [("row", 1), ("col", 1)]
    n_ex = len(links)
    quarter = half // 2
    r_low = r % 2

    def gram_half(which):
        return gfull.at[rows_at(which * half, half)]

    def gram_copy(e):
        axis, stride = links[e]
        row = flip(r, stride) if axis == "row" else r
        col = flip(c, stride) if axis == "col" else c
        if e == 0:
            src, dst = gram_half(1 - core), grecv.at[0]
        elif e in (1, n_ex - 1):
            src, dst = gsum.at[e - 1], grecv.at[e]
        elif e == 2:
            src, dst = gsum.at[1, rows_at((1 - r_low) * quarter, quarter)], grecv.at[2, :quarter]
        else:
            src, dst = gsum.at[e - 1, :quarter], grecv.at[e, :quarter]
        return remote(src, dst, g_send.at[e], g_recv.at[e], row, col)

    def gram_start():
        gfull[...] = lax.dot_general(
            fac[...], fac[...], (((0,), (0,)), ((), ())), preferred_element_type=F32
        )
        gram_copy(0).start()

    def gram_step(e):
        gram_copy(e - 1).wait_recv()
        if e == 1:
            gsum[0] = gram_half(core)[...] + grecv[0]
        elif e == 2:
            gsum[1] = gsum[0] + grecv[1]
        elif e == 3:
            gsum[2, :quarter] = gsum[1, rows_at(r_low * quarter, quarter)] + grecv[2, :quarter]
        elif e < n_ex - 1:
            gsum[e - 1, :quarter] = gsum[e - 2, :quarter] + grecv[e - 1, :quarter]
        else:
            gsum[e - 1, rows_at(r_low * quarter, quarter)] = gsum[e - 2, :quarter]
            gsum[e - 1, rows_at((1 - r_low) * quarter, quarter)] = grecv[e - 1, :quarter]
        gram_copy(e).start()

    def panel_rows(slot, start, count):
        return panel.at[pl.ds(pl.multiple_of(slot * own + start, part), count)]

    if n_row == 2:
        on_both = range(2 * ALONE, PARTS)
        on_own = [*range(ALONE), *on_both]
        on_twin = [*range(ALONE, 2 * ALONE), *on_both]

        def a_copy(q):
            return remote(
                fac.at[pl.ds(q * part, part)], panel_rows(a_slot, q * part, part),
                a_send.at[q], line_recv.at[a_slot, q], r, a_col,
            )

        def b_copy(q):
            return remote(
                fac.at[pl.ds(q * part, part)], stage.at[q], b_send.at[q], b_recv.at[q], 1 - r, c
            )

        def c_copy(q):
            return remote(
                stage.at[q], panel_rows(c_slot, q * part, part),
                c_send.at[q], line_recv.at[c_slot, q], r, c_col,
            )

        from_own = n_row * c // n_col == r
        near_at = jnp.where(from_own, 0, ALONE)

        def line_wait(j, q):
            remote(
                stage.at[0], panel_rows(j, q * part, part),
                c_send.at[0], line_recv.at[j, q], r, c,
            ).wait_recv()

        def x_copy(j, p, at):
            piece = panel_rows(j, (at + p) * part, part)
            return remote(piece, piece, x_send.at[j, p], x_recv.at[j, p], 1 - r, c)

        pl.semaphore_wait(barrier, sum(others))
        for q in on_twin:
            b_copy(q).start()

        @pl.when(a_col != c)
        def _():
            for q in on_own:
                a_copy(q).start()

        @pl.when(a_col == c)
        def _():
            for q in on_own:
                panel_rows(a_slot, q * part, part)[...] = fac[q * part : (q + 1) * part, :]

        gram_start()
        for n, q in enumerate(on_twin):
            b_copy(q).wait_recv()

            @pl.when(c_col != c)
            def _():
                c_copy(q).start()

            @pl.when(c_col == c)
            def _():
                panel_rows(c_slot, q * part, part)[...] = stage[q]

            if n == 1:
                gram_step(1)
        for p in range(ALONE):
            for j in range(n_row):
                @pl.when((n_row * c + j) % n_col != c)
                def _():
                    line_wait(j, near_at + p)

                x_copy(j, p, near_at).start()
        for q in on_both:
            for j in range(n_row):
                @pl.when((n_row * c + j) % n_col != c)
                def _():
                    line_wait(j, q)
        for p in range(ALONE):
            for j in range(n_row):
                x_copy(j, p, ALONE - near_at).wait_recv()
    else:
        def to_row(k):
            return remote(
                fac, panel_rows(a_slot, 0, own), a_send.at[k], x_recv.at[a_slot, 0],
                (r + k) % n_row, a_col,
            )

        @pl.when(a_col == c)
        def _():
            panel_rows(a_slot, 0, own)[...] = fac[...]

        @pl.when(a_col != c)
        def _():
            to_row(0).start()

        for k in range(1, n_row):
            to_row(k).start()
        gram_start()
        gram_step(1)
        for j in range(n_row):
            @pl.when(n_row * c + j != mine)
            def _():
                remote(
                    fac, panel_rows(j, 0, own), a_send.at[0], x_recv.at[j, 0], r, c
                ).wait_recv()

    def first(u):
        return remote(s1.at[u], r1.at[u], s1_send.at[u], s1_recv.at[u], r, flip(c, 1))

    def second(i):
        return remote(s2.at[i], r2.at[i], s2_send.at[i], s2_recv.at[i], r, flip(c, 2))

    def third(j, way, tgt, m):
        col = jnp.where(way == 0, c + 4, c - 4)
        return remote(
            s3.at[j], r3.at[way, tgt, m], s3_send.at[j], s3_recv.at[way, tgt, m], r, col
        )

    def diagonal(i, side, which):
        j = r * n_col + shard_of(i, side, which) - n_row * c

        @pl.when((j >= 0) & (j < n_row))
        def _():
            base = (j * own + i % nm * chunk) // LANES
            line = lax.broadcasted_iota(jnp.int32, (LANES, LANES), 0)
            lane = lax.broadcasted_iota(jnp.int32, (LANES, LANES), 1)
            for q in range(chunk // LANES):
                values = jnp.broadcast_to(diag[pl.ds(base + q, 1), :], (LANES, LANES))
                square = jnp.where(line == lane, values, 0.0).astype(BF16)
                acc[side, pl.ds(which * chunk + q * LANES, LANES), :] -= jnp.dot(
                    square, panel[rows_at((base + q) * LANES, LANES), :],
                    preferred_element_type=F32,
                )

    def pace(e):
        return 1 + PACE * (e - 2)

    def to_next(j):
        t, m = j // nm, j % nm
        tgt = target(t)
        way = jnp.where(tgt > hi, 0, 1)
        inner = jnp.where(way == 0, hi, n_hi - 1 - hi) > 0
        first(2 * j + 1).wait_recv()
        second(j).wait_recv()
        part_sum = keep[j] + r1[2 * j + 1].astype(F32) + r2[j].astype(F32)

        @pl.when(inner)
        def _():
            third(j, way, tgt, m).wait_recv()
            s3[j] = (part_sum + r3[way, tgt, m].astype(F32)).astype(BF16)

        @pl.when(jnp.logical_not(inner))
        def _():
            s3[j] = part_sum.astype(BF16)

        third(j, way, tgt, m).start()

    @pl.loop(0, steps)
    def _(i):
        for side in range(2):
            for which in range(2):
                fetch(i, side, which).wait()
            acc[side] = jnp.dot(tile[i % slots, side], panel[...], preferred_element_type=F32)

            @pl.when(i + slots < steps)
            def _():
                for which in range(2):
                    fetch(i + slots, side, which).start()

            for which in range(2):
                diagonal(i, side, which)
            s1[2 * i + side] = acc[side, :chunk, :].astype(BF16)
            first(2 * i + side).start()
        keep[i] = acc[1, chunk:, :]
        first(2 * i).wait_recv()
        s2[i] = (acc[0, chunk:, :] + r1[2 * i].astype(F32)).astype(BF16)
        second(i).start()

        @pl.when((i >= LAG) & (i - LAG < far))
        def _():
            to_next(i - LAG)

        for e in range(2, n_ex):
            if pace(e) < steps:
                @pl.when(i == pace(e))
                def _():
                    gram_step(e)

    for e in range(2, n_ex):
        if pace(e) >= steps:
            gram_step(e)

    if steps - LAG < far:
        @pl.loop(max(steps - LAG, 0), far)
        def _(j):
            to_next(j)

    gram_copy(n_ex - 1).wait_recv()
    gram_copy(0).wait_send()
    gram_half(core)[...] = gsum[n_ex - 2]
    gram_half(1 - core)[...] = grecv[n_ex - 1]
    total = gfull[...]
    total_hi = total.astype(BF16)
    total_lo = (total - total_hi.astype(F32)).astype(BF16)

    @pl.loop(0, nm)
    def _(m):
        rows = rows_at(m * chunk, chunk)
        model = jnp.dot(fac[rows, :], total_hi, preferred_element_type=F32)
        model += jnp.dot(fac[rows, :], total_lo, preferred_element_type=F32)
        result[rows, :] = model

    def put(m):
        rows = rows_at(m * chunk, chunk)
        return pltpu.make_async_copy(result.at[rows], out_ref.at[rows], out_sem.at[m])

    @pl.loop(0, nm)
    def _(m):
        j = far + m
        rows = rows_at(m * chunk, chunk)
        first(2 * j + 1).wait_recv()
        result[rows, :] -= keep[j] + r1[2 * j + 1].astype(F32)

        @pl.when(hi > 0)
        def _():
            third(0, 0, hi, m).wait_recv()
            result[rows, :] -= r3[0, hi, m].astype(F32)

        @pl.when(hi < n_hi - 1)
        def _():
            third(0, 1, hi, m).wait_recv()
            result[rows, :] -= r3[1, hi, m].astype(F32)

        second(j).wait_recv()
        result[rows, :] = 4.0 * (result[rows, :] - r2[j].astype(F32))
        put(m).start()

    if n_row == 2:
        for q in on_twin:
            b_copy(q).wait_send()

        @pl.when(a_col != c)
        def _():
            for q in on_own:
                a_copy(q).wait_send()

        @pl.when(c_col != c)
        def _():
            for q in on_twin:
                c_copy(q).wait_send()

        for p in range(ALONE):
            for j in range(n_row):
                x_copy(j, p, near_at).wait_send()
    else:
        @pl.when(a_col != c)
        def _():
            to_row(0).wait_send()

        for k in range(1, n_row):
            to_row(k).wait_send()
    for e in range(1, n_ex):
        gram_copy(e).wait_send()

    @pl.loop(0, steps)
    def _(i):
        first(2 * i).wait_send()
        first(2 * i + 1).wait_send()
        second(i).wait_send()

    @pl.loop(0, far)
    def _(j):
        tgt = target(j // nm)
        third(j, jnp.where(tgt > hi, 0, 1), tgt, j % nm).wait_send()

    @pl.loop(0, nm)
    def _(m):
        put(m).wait()


def local(ld_matrix, factor, diag_values):
    n_row, n_col = lax.axis_size("row"), lax.axis_size("col")
    own, rank = factor.shape
    width = ld_matrix.shape[1]
    n_hi = n_col // 4
    chunk = min(CHUNK, own)
    nm = own // chunk
    steps = n_hi * nm
    far = (n_hi - 1) * nm
    slots = min(SLOTS, steps)
    n_ex = n_col.bit_length() - 1 + n_row.bit_length() - 1 + 2
    dma = lambda *shape: pltpu.SemaphoreType.DMA(shape)
    sums = lambda *n: pltpu.VMEM((*n, chunk, rank), BF16)
    gram = pltpu.VMEM((n_ex, rank // 2, rank), F32)
    anywhere = pl.BlockSpec(memory_space=pl.ANY)
    own_barrier = dict(collective_id=0) if n_row == 2 else {}
    return pl.pallas_call(
        functools.partial(kernel, n_row, n_col, slots),
        out_shape=jax.ShapeDtypeStruct((own, rank), F32),
        in_specs=[anywhere, anywhere, pl.BlockSpec(memory_space=pltpu.VMEM)],
        out_specs=anywhere,
        scratch_shapes=[
            pltpu.VMEM((slots, 2, 2 * chunk, width), BF16),
            pltpu.VMEM((own, rank), F32),
            pltpu.VMEM((own, rank), BF16),
            pltpu.VMEM((width // LANES, LANES), F32),
            pltpu.VMEM((width, rank), BF16),
            pltpu.VMEM((PARTS, own // PARTS, rank), BF16),
            pltpu.VMEM((2, 2 * chunk, rank), F32),
            pltpu.VMEM((steps, chunk, rank), F32),
            pltpu.VMEM((own, rank), F32),
            sums(2 * steps), sums(2 * steps), sums(steps), sums(steps),
            sums(far), sums(2, n_hi, nm),
            gram, gram, pltpu.VMEM((rank, rank), F32),
            dma(slots, 2, 2), pltpu.SemaphoreType.DMA, dma(nm),
            dma(PARTS), dma(PARTS), dma(PARTS), dma(PARTS),
            dma(n_row, PARTS), dma(n_row, PARTS), dma(n_row, PARTS),
            dma(2 * steps), dma(2 * steps), dma(steps), dma(steps),
            dma(far), dma(2, n_hi, nm), dma(n_ex), dma(n_ex),
        ],
        compiler_params=pltpu.CompilerParams(
            has_side_effects=True, vmem_limit_bytes=63 * 2**20, **own_barrier
        ),
    )(ld_matrix, factor, diag_values.reshape(width // LANES, LANES))


def solution(mesh):
    in_specs = (P("row", "col"), P(("row", "col"), None), P("col"))
    out_specs = P(("row", "col"), None)
    return jax.shard_map(local, mesh=mesh, in_specs=in_specs, out_specs=out_specs, check_vma=False)
```

time: 99.8 us -> 80.8 us (0.81)
  Pallas kernels: 95.2 us -> 78.4 us
  local copies, waits for them, and re-layouts: 3.55 us -> 2.26 us
    pallas_call x1, Pallas kernels: 95.2 us -> 78.4 us  [local(): pl.pallas_call(functools.partial(kernel, n_row, n_col, slots), out_shape=...]
    broadcast_in_dim x1 -> x0, local copies, waits for them, and re-layouts: 1.29 us -> none  [local(): diag_values[None, :]]
where the time goes in v2:
time: 80.8 us; the launch traced here: 80.6 us
  Pallas kernels  78.4 us (97%)
  local copies, waits for them, and re-layouts  2.26 us (3%)
    pallas_call x1, Pallas kernels, local(): pl.pallas_call(functools.partial(kernel, n_row, n_col, slots), out_shape=...  78.4 us
    unnamed x1, local copies, waits for them, and re-layouts  2.26 us

profile of v2, /device:TPU:0, one launch (start us, length us, event | category | flops | bytes accessed | tf_op | source)
XLA Modules:
  0.0 80.6 jit_solution(14650199073884402141)
XLA Ops:
  0.0 78.4 %shard_map.37 = f32[1024,256]{1,0:T(8,128)} custom-call(bf16[16384,2048]{1,0:T(8,128)(2,1)} %ld_ref.1, f32[1024,256]{1,0:T(8,128)} %f32_ref.1, bf16[16,128]{1,0:T(8,128)(2,1)} %bitcast.1), custom_call_target="tpu_custom_call" | custom-call | tf_op jit(solution)/shard_map/pallas_call | solution.py:447
  78.4 2.3 %copy.5 = f32[1024,256]{1,0:T(8,128)} copy(f32[1024,256]{1,0:T(8,128)} %shard_map.37) | data formatting | bytes 2097152

commit v3 on v2

--- a/solution.py
+++ b/solution.py
@@ -11,10 +11,10 @@
 F32, BF16 = jnp.float32, jnp.bfloat16
 CHUNK = 256
 LAG = 3
-PACE = 3
+PACE = 4
 SLOTS = 6
 PARTS = 16
-ALONE = 4
+OWN, TWIN = 4, 4
 LANES = 128
 
 
@@ -151,9 +151,9 @@
         return panel.at[pl.ds(pl.multiple_of(slot * own + start, part), count)]
 
     if n_row == 2:
-        on_both = range(2 * ALONE, PARTS)
-        on_own = [*range(ALONE), *on_both]
-        on_twin = [*range(ALONE, 2 * ALONE), *on_both]
+        own_only, twin_only = range(OWN), range(OWN, OWN + TWIN)
+        on_both = range(OWN + TWIN, PARTS)
+        on_own, on_twin = [*own_only, *on_both], [*twin_only, *on_both]
 
         def a_copy(q):
             return remote(
@@ -173,7 +173,6 @@
             )
 
         from_own = n_row * c // n_col == r
-        near_at = jnp.where(from_own, 0, ALONE)
 
         def line_wait(j, q):
             remote(
@@ -181,9 +180,26 @@
                 c_send.at[0], line_recv.at[j, q], r, c,
             ).wait_recv()
 
-        def x_copy(j, p, at):
-            piece = panel_rows(j, (at + p) * part, part)
-            return remote(piece, piece, x_send.at[j, p], x_recv.at[j, p], 1 - r, c)
+        def x_copy(j, q):
+            piece = panel_rows(j, q * part, part)
+            return remote(piece, piece, x_send.at[j, q], x_recv.at[j, q], 1 - r, c)
+
+        def from_line(j, q):
+            @pl.when((n_row * c + j) % n_col != c)
+            def _():
+                line_wait(j, q)
+
+        def meet(here, there):
+            for q in here:
+                for j in range(n_row):
+                    from_line(j, q)
+                    x_copy(j, q).start()
+            for q in on_both:
+                for j in range(n_row):
+                    from_line(j, q)
+            for q in there:
+                for j in range(n_row):
+                    x_copy(j, q).wait_recv()
 
         pl.semaphore_wait(barrier, sum(others))
         for q in on_twin:
@@ -213,21 +229,14 @@
 
             if n == 1:
                 gram_step(1)
-        for p in range(ALONE):
-            for j in range(n_row):
-                @pl.when((n_row * c + j) % n_col != c)
-                def _():
-                    line_wait(j, near_at + p)
-
-                x_copy(j, p, near_at).start()
-        for q in on_both:
-            for j in range(n_row):
-                @pl.when((n_row * c + j) % n_col != c)
-                def _():
-                    line_wait(j, q)
-        for p in range(ALONE):
-            for j in range(n_row):
-                x_copy(j, p, ALONE - near_at).wait_recv()
+
+        @pl.when(from_own)
+        def _():
+            meet(own_only, twin_only)
+
+        @pl.when(jnp.logical_not(from_own))
+        def _():
+            meet(twin_only, own_only)
     else:
         def to_row(k):
             return remote(
@@ -399,9 +408,12 @@
             for q in on_twin:
                 c_copy(q).wait_send()
 
-        for p in range(ALONE):
-            for j in range(n_row):
-                x_copy(j, p, near_at).wait_send()
+        for here, gone in ((from_own, own_only), (jnp.logical_not(from_own), twin_only)):
+            @pl.when(here)
+            def _():
+                for q in gone:
+                    for j in range(n_row):
+                        x_copy(j, q).wait_send()
     else:
         @pl.when(a_col != c)
         def _():

time: 80.8 us -> 79.9 us (0.989)
  Pallas kernels: 78.4 us -> 76.9 us
    pallas_call x1, Pallas kernels: 78.4 us -> 76.9 us  [local(): pl.pallas_call(functools.partial(kernel, n_row, n_col, slots), out_shape=...]
where the time goes in v3:
time: 79.9 us; the launch traced here: 79.2 us
  Pallas kernels  76.9 us (96%)
  local copies, waits for them, and re-layouts  2.26 us (3%)
    pallas_call x1, Pallas kernels, local(): pl.pallas_call(functools.partial(kernel, n_row, n_col, slots), out_shape=...  76.9 us
    unnamed x1, local copies, waits for them, and re-layouts  2.26 us

profile of v3, /device:TPU:0, one launch (start us, length us, event | category | flops | bytes accessed | tf_op | source)
XLA Modules:
  0.0 79.2 jit_solution(6989551227615024253)
XLA Ops:
  0.0 76.9 %shard_map.37 = f32[1024,256]{1,0:T(8,128)} custom-call(bf16[16384,2048]{1,0:T(8,128)(2,1)} %ld_ref.1, f32[1024,256]{1,0:T(8,128)} %f32_ref.1, bf16[16,128]{1,0:T(8,128)(2,1)} %bitcast.1), custom_call_target="tpu_custom_call" | custom-call | tf_op jit(solution)/shard_map/pallas_call | solution.py:459
  77.0 2.3 %copy.5 = f32[1024,256]{1,0:T(8,128)} copy(f32[1024,256]{1,0:T(8,128)} %shard_map.37) | data formatting | bytes 2097152
